TPU v7x, 8 devices: a whole 2x2x1 slice. The times are simulated.
8 devices in a mesh: dp: 1 (over z), tp: 8 (over x, y, core).
Axes of the slice: x: 2, y: 2, z: 1, core: 2. Of those that a mesh axis runs over, the one named last changes fastest.
Arguments:
- x: bfloat16 [1024, 8192], P(('dp', 'tp'))
- w_gate: bfloat16 [8192, 28672], P(None, 'tp')
- w_up: bfloat16 [8192, 28672], P(None, 'tp')
- w_down: bfloat16 [28672, 8192], P('tp')
Outputs:
- output: bfloat16 [1024, 8192], P(('dp', 'tp'))
All inputs are finite; a program needn't handle non-finite values.
Results may differ from a plain program's by a relative error of at most 0.016.
Values are sent between devices in bfloat16 or wider.
A program may use at most 2 GiB of HBM per device.

v0:
```python
import jax
import jax.numpy as jnp
from jax import lax
from jax.sharding import PartitionSpec as P


def solution(mesh):
    def step(x, w_gate, w_up, w_down):
        rows = lax.all_gather(x, "tp", axis=0, tiled=True)
        gate = jnp.dot(rows, w_gate, preferred_element_type=jnp.float32)
        up = jnp.dot(rows, w_up, preferred_element_type=jnp.float32)
        hidden = (jax.nn.silu(gate) * up).astype(jnp.bfloat16)
        term = jnp.dot(hidden, w_down, preferred_element_type=jnp.float32).astype(jnp.bfloat16)
        return lax.psum_scatter(term, "tp", scatter_dimension=0, tiled=True)

    return jax.shard_map(
        step,
        mesh=mesh,
        in_specs=(P(("dp", "tp"), None), P(None, "tp"), P(None, "tp"), P("tp", None)),
        out_specs=P(("dp", "tp"), None),
        check_vma=False,
    )
```

profile of v0, /device:TPU:0, one launch (start us, length us, event | category | flops | bytes accessed | tf_op | source)
XLA Modules:
  0.0 419.9 jit_solution(16947859562751393140)
XLA Ops:
  6.5 0.0 all-gather.2.cloned.1.call-start
  6.5 0.7 all-gather.2.cloned.1.call-update
  7.3 0.0 reduce-scatter.2.cloned.1.call-start
  7.3 88.8 %all-gather.2.cloned.1.call-done = bf16[1024,8192]{1,0:T(8,128)(2,1)} async-done(((bf16[128,8192]{1,0:T(8,128)(2,1)}), bf16[1024,8192]{1,0:T(8,128)(2,1)}) %all-gather.2.cloned.1.call-update) | async-done | bytes 16777232 | tf_op jit(solution)/shard_map/all_gather | solution.py:9
  96.1 71.3 %fusion = f32[1024,3584]{1,0:T(8,128)} fusion(bf16[1024,8192]{1,0:T(8,128)(2,1)} %all-gather.2.cloned.1.call-done, bf16[8192,3584]{1,0:T(8,128)(2,1)} %param.5), kind=kOutput, calls=%fused_computation.2 | convolution fusion | flops 60129542144 | bytes 90177536 | tf_op jit(solution)/shard_map/dot_general | solution.py:10
  167.3 72.1 %multiply_convert_fusion = bf16[1024,3584]{1,0:T(8,128)(2,1)S(1)} fusion(f32[1024,3584]{1,0:T(8,128)} %fusion, bf16[1024,8192]{1,0:T(8,128)(2,1)} %all-gather.2.cloned.1.call-done, bf16[8192,3584]{1,0:T(8,128)(2,1)} %param.6), kind=kOutput, calls=%fused_computation.1 | convolution fusion | flops 60151562240 | bytes 97517568 | tf_op jit(solution)/shard_map/dot_general | solution.py:11
  239.4 66.5 %convolution_convert_fusion = bf16[1024,8192]{1,0:T(8,128)(2,1)} fusion(bf16[1024,3584]{1,0:T(8,128)(2,1)S(1)} %multiply_convert_fusion, bf16[3584,8192]{1,0:T(8,128)(2,1)} %param.7), kind=kOutput, calls=%fused_computation | convolution fusion | flops 60137930752 | bytes 82837504 | tf_op jit(solution)/shard_map/dot_general | solution.py:13
  305.9 0.0 reduce-scatter.2.cloned.1.call-update
  305.9 107.1 %reduce-scatter.2.cloned.1.call-done = bf16[128,8192]{1,0:T(8,128)(2,1)} async-done(((bf16[1024,8192]{1,0:T(8,128)(2,1)}), bf16[128,8192]{1,0:T(8,128)(2,1)}) %reduce-scatter.2.cloned.1.call-update) | async-done | bytes 2097168 | tf_op jit(solution)/shard_map/reduce_scatter | solution.py:14
Async XLA Ops:
  6.5 89.6 %all-gather.2.cloned.1.call-start = ((), (), s32[]{:S(2)}) async-start(), calls=%async_computation.1 | async-start | bytes 18874368 | tf_op jit(solution)/shard_map/all_gather | solution.py:9
  7.3 405.8 %reduce-scatter.2.cloned.1.call-start = ((), (), s32[]{:S(2)}) async-start(), calls=%async_computation.2 | async-start | bytes 18874368 | tf_op jit(solution)/shard_map/reduce_scatter | solution.py:14
Sparse Core Ops, SparseCore 0:
  9.1 86.8 all-gather.1
  306.0 106.9 reduce-scatter.1
where the time goes:
time: 420 us
  matrix products  210 us (50%)
  waiting for transfers between devices  197 us (47%)
  between operations  13.4 us (3%)
    reduce_scatter x1, waiting for transfers between devices, step(): return lax.psum_scatter(term, 'tp', scatter_dimension=0, tiled=True)  107 us
    all_gather x1, waiting for transfers between devices, step(): rows = lax.all_gather(x, 'tp', axis=0, tiled=True)  88.8 us
    dot_general x1, matrix products, step(): up = jnp.dot(rows, w_up, preferred_element_type=jnp.float32)  72.1 us
    dot_general x1, matrix products, step(): gate = jnp.dot(rows, w_gate, preferred_element_type=jnp.float32)  71.3 us
    dot_general x1, matrix products, step(): jnp.dot(hidden, w_down, preferred_element_type=jnp.float32)  66.5 us
  transfers between devices with their start and end apart: 2, of which 2 were waited for; matrix products, arithmetic and copies ran while one was open for 0% of the time, Pallas kernels for 0%

commit v1 on v0

v1 whole, which is shorter than its diff:
```python
import functools

import jax
import jax.numpy as jnp
from jax import lax
from jax.experimental import pallas as pl
from jax.experimental.pallas import tpu as pltpu
from jax.sharding import PartitionSpec as P

F32, BF16 = jnp.float32, jnp.bfloat16
HALVES = 2
TILE = 256
WIDE = 512
CHUNKS = 8
EARLY = 7
SLOTS = 4
OWN = 7


def kernel(
    x_hbm, wg_hbm, wu_hbm, wd_hbm, y_hbm,
    xv, hid, ring, acc, send0, recv0, send1, recv1, send2, recv2, ost,
    wsem, xsem, osem, ag_s, ag_r, s0, r0, s1, r1, s2, r2, free0, free1, free2,
):
    rows = x_hbm.shape[0] // HALVES
    depth = x_hbm.shape[1]
    hidden = hid.shape[1]
    kc = depth // CHUNKS
    tiles = hidden // TILE
    late = tiles - EARLY
    pair = 2 * WIDE
    downs = depth // pair
    gathers = HALVES * CHUNKS
    sums = HALVES * downs
    group = 4 * rows

    me = lax.axis_index("tp")
    part = me + 1 - 2 * (me % 2)
    ynb = me + 2 - 4 * ((me // 2) % 2)
    xnb = (me + 4) % 8

    def rcopy(src, dst, ss, rs, dev):
        return pltpu.make_async_remote_copy(
            src_ref=src, dst_ref=dst, send_sem=ss, recv_sem=rs,
            device_id={"tp": dev}, device_id_type=pl.DeviceIdType.MESH,
        )

    def piece(q, block, lo, n):
        return xv.at[q // CHUNKS, pl.ds(block * rows + lo, n), pl.ds(pl.multiple_of((q % CHUNKS) * kc, kc), kc)]

    def ag(q, i, src, dst, dev):
        return rcopy(src, dst, ag_s.at[q, i], ag_r.at[q, i], dev)

    def ag_x(q):
        return ag(q, 0, piece(q, 0, 0, rows), piece(q, 2, 0, rows), xnb)

    def ag_y(q):
        return ag(q, 1, piece(q, 0, 0, rows), piece(q, 1, 0, rows), ynb)

    def ag_part(q, b):
        return ag(q, 2 + b, piece(q, b, 0, rows), piece(q, 4 + b, 0, rows), part)

    def ag_relay_y(q):
        return ag(q, 6, piece(q, 2, 0, rows // 2), piece(q, 3, 0, rows // 2), ynb)

    def ag_relay_x(q):
        return ag(q, 7, piece(q, 1, rows // 2, rows // 2), piece(q, 3, rows // 2, rows // 2), xnb)

    def gather_send(q):
        ag_x(q).start()
        ag_y(q).start()
        ag_part(q, 0).start()

    def gather_relay(q):
        ag_x(q).wait_recv()
        ag_relay_y(q).start()
        ag_y(q).wait_recv()
        ag_relay_x(q).start()
        ag_part(q, 2).start()
        ag_part(q, 1).start()

    def gather_diag(q):
        ag_relay_y(q).wait_recv()
        ag_relay_x(q).wait_recv()
        ag_part(q, 3).start()

    def gather_ready(q):
        for b in range(4):
            ag_part(q, b).wait_recv()

    def gather_sent(q):
        for c in (ag_x(q), ag_y(q), ag_relay_y(q), ag_relay_x(q), *(ag_part(q, b) for b in range(4))):
            c.wait_send()

    def w_early(t, slot):
        ks = pl.ds(pl.multiple_of(t * kc, kc), kc)
        out = []
        for n in range(EARLY):
            for j, w in enumerate((wg_hbm, wu_hbm)):
                dst = ring.at[slot, pl.ds(n * kc, kc), pl.ds(j * TILE, TILE)]
                out.append(pltpu.make_async_copy(w.at[ks, pl.ds(n * TILE, TILE)], dst, wsem.at[slot, 2 * n + j]))
        return out

    def w_full(t, slot):
        cols = pl.ds(pl.multiple_of(t * TILE, TILE), TILE)
        return [
            pltpu.make_async_copy(w.at[:, cols], ring.at[slot, :, pl.ds(j * TILE, TILE)], wsem.at[slot, j])
            for j, w in enumerate((wg_hbm, wu_hbm))
        ]

    def w_down(t, slot):
        return [
            pltpu.make_async_copy(
                wd_hbm.at[:, pl.ds(pl.multiple_of(t * pair + b * WIDE, WIDE), WIDE)],
                ring.at[slot, pl.ds(b * hidden, hidden), :],
                wsem.at[slot, b],
            )
            for b in range(2)
        ]

    def start(copies):
        for c in copies:
            c.start()

    def wait(copies):
        for c in copies:
            c.wait()

    def to_part(u):
        s = u % SLOTS
        return rcopy(send0.at[s], recv0.at[s], s0.at[s], r0.at[s], part)

    def to_first(u, b):
        s = u % SLOTS
        return rcopy(send1.at[s, b], recv1.at[s, b], s1.at[s, b], r1.at[s, b], (xnb, ynb)[b])

    def to_second(u, b):
        s = u % SLOTS
        return rcopy(send2.at[s, b], recv2.at[s, b], s2.at[s, b], r2.at[s, b], (ynb, xnb)[b])

    def out_copy(u):
        cols = pl.ds(pl.multiple_of((u % downs) * pair, pair), pair)
        return pltpu.make_async_copy(ost.at[u % 2], y_hbm.at[pl.ds((u // downs) * rows, rows), cols], osem.at[u % 2])

    def credit(sem, u, dev):
        @pl.when(u + SLOTS < sums)
        def _():
            pl.semaphore_signal(sem, inc=1, device_id={"tp": dev}, device_id_type=pl.DeviceIdType.MESH)

    def spend(sem, u):
        @pl.when(u >= SLOTS)
        def _():
            pl.semaphore_wait(sem, 1)

    def sum_first(u):
        s, o = u % SLOTS, u % OWN
        to_part(u).wait_recv()

        @pl.when(u >= SLOTS)
        def _():
            for b in range(2):
                to_first(u - SLOTS, b).wait_send()

        for b in range(2):
            cols = pl.ds(b * WIDE, WIDE)
            keep = (1, 2)[b]
            go = (2, 1)[b]
            for blk in (0, keep):
                at = pl.ds(b * group + blk * rows, rows)
                acc[o, at, :] += recv0[s, pl.ds(blk * rows, rows), cols].astype(F32)
            for i, blk in enumerate((go, 3)):
                at = pl.ds(b * group + blk * rows, rows)
                total = acc[o, at, :] + recv0[s, pl.ds(blk * rows, rows), cols].astype(F32)
                send1[s, b, pl.ds(i * rows, rows), :] = total.astype(BF16)
        credit(free0, u, part)
        for b in range(2):
            spend(free1.at[b], u)
            to_first(u, b).start()

    def sum_second(u):
        s, o = u % SLOTS, u % OWN
        for b in range(2):
            to_first(u, b).wait_recv()

        @pl.when(u >= SLOTS)
        def _():
            for b in range(2):
                to_second(u - SLOTS, b).wait_send()

        for b in range(2):
            keep = (1, 2)[b]
            mine = pl.ds(b * group, rows)
            acc[o, mine, :] += recv1[s, b, pl.ds(0, rows), :].astype(F32)
            total = acc[o, pl.ds(b * group + keep * rows, rows), :] + recv1[s, b, pl.ds(rows, rows), :].astype(F32)
            send2[s, b] = total.astype(BF16)
        for b in range(2):
            credit(free1.at[b], u, (xnb, ynb)[b])
            spend(free2.at[b], u)
            to_second(u, b).start()

    def sum_last(u):
        s, o = u % SLOTS, u % OWN
        for b in range(2):
            to_second(u, b).wait_recv()

        @pl.when(u >= 2)
        def _():
            out_copy(u - 2).wait()

        for b in range(2):
            total = acc[o, pl.ds(b * group, rows), :] + recv2[s, b].astype(F32)
            ost[u % 2, :, pl.ds(b * WIDE, WIDE)] = total.astype(BF16)
        for b in range(2):
            credit(free2.at[b], u, (ynb, xnb)[b])
        out_copy(u).start()

    def sums_at(v, lo):
        for lag, stage in ((1, sum_first), (3, sum_second), (5, sum_last)):
            u = v - lag

            @pl.when((u >= lo) & (u < lo + downs))
            def _():
                stage(u)

    def gated(gate, up):
        return (jax.nn.silu(gate) * up).astype(BF16)

    own = [
        pltpu.make_async_copy(x_hbm.at[pl.ds(h * rows, rows), :], xv.at[h, pl.ds(0, rows), :], xsem.at[h])
        for h in range(HALVES)
    ]
    start(own)
    start(w_early(0, 0))
    barrier = pltpu.get_barrier_semaphore()
    for dev in (part, ynb, xnb):
        pl.semaphore_signal(barrier, inc=1, device_id={"tp": dev}, device_id_type=pl.DeviceIdType.MESH)
    acc[...] = jnp.zeros_like(acc)
    pl.semaphore_wait(barrier, 3)
    wait(own)
    for q in range(2):
        gather_send(q)
    gather_relay(0)
    gather_send(2)
    gather_diag(0)

    def gather_at(g):
        @pl.when((g >= 1) & (g < gathers))
        def _():
            gather_diag(g)

        @pl.when(g + 1 < gathers)
        def _():
            gather_relay(g + 1)

        @pl.when(g + 3 < gathers)
        def _():
            gather_send(g + 3)

    def early_trip(t, _):
        slot = t % 2
        gather_at(t)
        wait(w_early(t, slot))

        @pl.when(t + 1 < CHUNKS)
        def _():
            start(w_early(t + 1, 1 - slot))

        @pl.when(t + 1 == CHUNKS)
        def _():
            start(w_full(EARLY, 1 - slot))

        gather_ready(t)
        for n in range(EARLY):
            acc[n] += jnp.dot(
                xv[0, :, pl.ds(pl.multiple_of(t * kc, kc), kc)],
                ring[slot, n * kc : (n + 1) * kc, :],
                preferred_element_type=F32,
            )
        return 0

    lax.fori_loop(0, CHUNKS, early_trip, 0)

    def full_tile(h, t, slot):
        r = jnp.dot(xv[h], ring[slot], preferred_element_type=F32)
        hid[:, pl.ds(pl.multiple_of(t * TILE, TILE), TILE)] = gated(r[:, :TILE], r[:, TILE:])

    base = CHUNKS

    def late_trip(t, _):
        slot = (base + t) % 2
        gather_at(CHUNKS + t)
        wait(w_full(EARLY + t, slot))

        @pl.when(t + 1 < late)
        def _():
            start(w_full(EARLY + t + 1, 1 - slot))

        @pl.when(t + 1 == late)
        def _():
            start(w_down(0, 1 - slot))

        full_tile(0, EARLY + t, slot)
        a = acc[t]
        hid[:, pl.ds(pl.multiple_of(t * TILE, TILE), TILE)] = gated(a[:, :TILE], a[:, TILE:])
        return 0

    lax.fori_loop(0, late, late_trip, 0)
    base += late
    for q in range(base, gathers):
        gather_diag(q)

    def down_loop(h, base, lo):
        def trip(t, _):
            slot = (base + t) % 2
            u = lo + t
            sums_at(u, lo)
            wait(w_down(t, slot))

            @pl.when(t + 1 < downs)
            def _():
                start(w_down(t + 1, 1 - slot))

            if h + 1 < HALVES:

                @pl.when(t + 1 == downs)
                def _():
                    start(w_full(0, 1 - slot))

            @pl.when(u >= SLOTS)
            def _():
                to_part(u - SLOTS).wait_send()

            s, o = u % SLOTS, u % OWN
            for b in range(2):
                r = jnp.dot(hid[...], ring[slot, b * hidden : (b + 1) * hidden, :], preferred_element_type=F32)
                acc[o, pl.ds(b * group, group), :] = r[:group]
                send0[s, :, b * WIDE : (b + 1) * WIDE] = r[group:].astype(BF16)
            spend(free0, u)
            to_part(u).start()
            return 0

        lax.fori_loop(0, downs, trip, 0)

    down_loop(0, base, 0)
    base += downs

    def drain(q, _):
        gather_ready(q)
        return 0

    lax.fori_loop(CHUNKS, gathers, drain, 0)

    def full_trip(t, _):
        slot = (base + t) % 2
        sums_at(downs + t, 0)
        wait(w_full(t, slot))

        @pl.when(t + 1 < tiles)
        def _():
            start(w_full(t + 1, 1 - slot))

        @pl.when(t + 1 == tiles)
        def _():
            start(w_down(0, 1 - slot))

        full_tile(1, t, slot)
        return 0

    lax.fori_loop(0, tiles, full_trip, 0)
    down_loop(1, base + tiles, downs)

    def tail(v, _):
        sums_at(v, downs)
        return 0

    lax.fori_loop(sums, sums + 5, tail, 0)

    def sent(q, _):
        gather_sent(q)
        return 0

    lax.fori_loop(0, gathers, sent, 0)

    def last(u, _):
        to_part(u).wait_send()
        for b in range(2):
            to_first(u, b).wait_send()
            to_second(u, b).wait_send()
        return 0

    lax.fori_loop(sums - SLOTS, sums, last, 0)
    for u in (sums - 2, sums - 1):
        out_copy(u).wait()


def solution(mesh):
    def step(x, w_gate, w_up, w_down):
        n = mesh.shape["tp"]
        rows, depth = x.shape
        hidden = w_gate.shape[1]
        m = n * rows // HALVES
        r = rows // HALVES
        gathers = HALVES * CHUNKS
        dma = pltpu.SemaphoreType.DMA
        return pl.pallas_call(
            kernel,
            out_shape=jax.ShapeDtypeStruct((rows, depth), BF16),
            in_specs=[pl.BlockSpec(memory_space=pltpu.HBM)] * 4,
            out_specs=pl.BlockSpec(memory_space=pltpu.HBM),
            scratch_shapes=[
                pltpu.VMEM((HALVES, m, depth), BF16),
                pltpu.VMEM((m, hidden), BF16),
                pltpu.VMEM((2, depth, 2 * TILE), BF16),
                pltpu.VMEM((EARLY, m, 2 * TILE), F32),
                pltpu.VMEM((SLOTS, 4 * r, 2 * WIDE), BF16),
                pltpu.VMEM((SLOTS, 4 * r, 2 * WIDE), BF16),
                pltpu.VMEM((SLOTS, 2, 2 * r, WIDE), BF16),
                pltpu.VMEM((SLOTS, 2, 2 * r, WIDE), BF16),
                pltpu.VMEM((SLOTS, 2, r, WIDE), BF16),
                pltpu.VMEM((SLOTS, 2, r, WIDE), BF16),
                pltpu.VMEM((2, r, 2 * WIDE), BF16),
                dma((2, 2 * EARLY)),
                dma((HALVES,)),
                dma((2,)),
                dma((gathers, 8)),
                dma((gathers, 8)),
                dma((SLOTS,)),
                dma((SLOTS,)),
                dma((SLOTS, 2)),
                dma((SLOTS, 2)),
                dma((SLOTS, 2)),
                dma((SLOTS, 2)),
                pltpu.SemaphoreType.REGULAR,
                pltpu.SemaphoreType.REGULAR((2,)),
                pltpu.SemaphoreType.REGULAR((2,)),
            ],
            compiler_params=pltpu.CompilerParams(
                collective_id=0, has_side_effects=True, vmem_limit_bytes=67043328
            ),
        )(x, w_gate, w_up, w_down)

    return jax.shard_map(
        step,
        mesh=mesh,
        in_specs=(P(("dp", "tp"), None), P(None, "tp"), P(None, "tp"), P("tp", None)),
        out_specs=P(("dp", "tp"), None),
        check_vma=False,
    )
```

time: 420 us -> 261 us (0.62)
  Pallas kernels: 0 us -> 258 us
  matrix products: 210 us -> 0 us
  waiting for transfers between devices: 197 us -> 0 us
  between operations: 13.4 us -> 0.01 us
    pallas_call x0 -> x1, Pallas kernels: none -> 258 us  [step(): pl.pallas_call(kernel, out_shape=jax.ShapeDtypeStruct((rows, depth), BF16...]
    dot_general x3 -> x0, matrix products: 210 us -> none  [the longest x1 72.1 us: step(): up = jnp.dot(rows, w_up, preferred_element_type=jnp.float32)]
    reduce_scatter x1 -> x0, waiting for transfers between devices: 107 us -> none  [step(): return lax.psum_scatter(term, 'tp', scatter_dimension=0, tiled=True)]
    all_gather x1 -> x0, waiting for transfers between devices: 88.8 us -> none  [step(): rows = lax.all_gather(x, 'tp', axis=0, tiled=True)]
  transfers between devices with their start and end apart: 2 -> 0, of which waited for: 2 -> 0; matrix products, arithmetic and copies ran while one was open for 0% -> 0% of each run, Pallas kernels for 0% -> 0%
where the time goes in v1:
time: 261 us
  Pallas kernels  258 us (99%)
  local copies, waits for them, and re-layouts  3.1 us (1%)
    pallas_call x1, Pallas kernels, step(): pl.pallas_call(kernel, out_shape=jax.ShapeDtypeStruct((rows, depth), BF16...  258 us

profile of v1, /device:TPU:0, one launch (start us, length us, event | category | flops | bytes accessed | tf_op | source)
XLA Modules:
  0.0 260.8 jit_solution(10993147031171847133)
XLA Ops:
  0.0 257.7 %shard_map.46 = bf16[128,8192]{1,0:T(8,128)(2,1)} custom-call(bf16[128,8192]{1,0:T(8,128)(2,1)} %x_hbm.1, bf16[8192,3584]{1,0:T(8,128)(2,1)} %wg_hbm.1, bf16[8192,3584]{1,0:T(8,128)(2,1)} %wu_hbm.1, bf16[3584,8192]{1,0:T(8,128)(2,1)} %wd_hbm.1), custom_call_target="tpu_custom_call" | custom-call | tf_op jit(solution)/shard_map/pallas_call | solution.py:405
  257.7 3.1 %copy.6 = bf16[128,8192]{1,0:T(8,128)(2,1)} copy(bf16[128,8192]{1,0:T(8,128)(2,1)} %shard_map.46) | data formatting | bytes 4194304

commit v2 on v0

v2 whole, which is shorter than its diff:
```python
import functools

import jax
import jax.numpy as jnp
from jax import lax
from jax.experimental import pallas as pl
from jax.experimental.pallas import tpu as pltpu
from jax.sharding import PartitionSpec as P

F32, BF16 = jnp.float32, jnp.bfloat16
HALVES = 2
TILE = 256
WIDE = 512
CHUNKS = (16, 8)
SLOTS = 5
OWN = 12


def kernel(
    x_hbm, wg_hbm, wu_hbm, wd_hbm, y_hbm,
    xv, hid, ring, acc, send0, recv0, send1, recv1, send2, recv2, ost,
    wsem, xsem, osem, ag_s, ag_r, s0, r0, s1, r1, s2, r2, free0, free1, free2,
):
    rows = x_hbm.shape[0] // HALVES
    depth = x_hbm.shape[1]
    hidden = hid.shape[1]
    kcs = [depth // n for n in CHUNKS]
    tiles = hidden // TILE
    blocks = hidden // WIDE
    pair = 2 * WIDE
    downs = depth // pair
    sums = HALVES * downs
    group = 4 * rows

    me = lax.axis_index("tp")
    part = me + 1 - 2 * (me % 2)
    ynb = me + 2 - 4 * ((me // 2) % 2)
    xnb = (me + 4) % 8

    def rcopy(src, dst, ss, rs, dev):
        return pltpu.make_async_remote_copy(
            src_ref=src, dst_ref=dst, send_sem=ss, recv_sem=rs,
            device_id={"tp": dev}, device_id_type=pl.DeviceIdType.MESH,
        )

    def piece(h, c, block, lo, n):
        return xv.at[h, pl.ds(block * rows + lo, n), pl.ds(pl.multiple_of(c * kcs[h], kcs[h]), kcs[h])]

    def ag(h, c, i, src, dst, dev):
        q = h * CHUNKS[0] + c
        return rcopy(piece(h, c, *src), piece(h, c, *dst), ag_s.at[q, i], ag_r.at[q, i], dev)

    def ag_x(h, c):
        return ag(h, c, 0, (0, 0, rows), (2, 0, rows), xnb)

    def ag_y(h, c):
        return ag(h, c, 1, (0, 0, rows), (1, 0, rows), ynb)

    def ag_part(h, c, b):
        return ag(h, c, 2 + b, (b, 0, rows), (4 + b, 0, rows), part)

    def ag_relay_y(h, c):
        return ag(h, c, 6, (2, 0, rows // 2), (3, 0, rows // 2), ynb)

    def ag_relay_x(h, c):
        return ag(h, c, 7, (1, rows // 2, rows // 2), (3, rows // 2, rows // 2), xnb)

    def gather_send(h, c):
        ag_x(h, c).start()
        ag_y(h, c).start()
        ag_part(h, c, 0).start()

    def gather_relay(h, c):
        ag_x(h, c).wait_recv()
        ag_relay_y(h, c).start()
        ag_y(h, c).wait_recv()
        ag_relay_x(h, c).start()
        ag_part(h, c, 2).start()
        ag_part(h, c, 1).start()

    def gather_diag(h, c):
        ag_relay_y(h, c).wait_recv()
        ag_relay_x(h, c).wait_recv()
        ag_part(h, c, 3).start()

    def gather_ready(h, c):
        for b in range(4):
            ag_part(h, c, b).wait_recv()

    def gather_sent(h, c):
        parts = [ag_part(h, c, b) for b in range(4)]
        for copy in (ag_x(h, c), ag_y(h, c), ag_relay_y(h, c), ag_relay_x(h, c), *parts):
            copy.wait_send()

    def w_chunk(t, slot):
        ks = pl.ds(pl.multiple_of(t * kcs[0], kcs[0]), kcs[0])
        return [
            pltpu.make_async_copy(
                w.at[ks, pl.ds(n * WIDE, WIDE)],
                ring.at[slot, pl.ds((j * blocks + n) * kcs[0], kcs[0]), :],
                wsem.at[slot],
            )
            for j, w in enumerate((wg_hbm, wu_hbm))
            for n in range(blocks)
        ]

    def w_full(t, slot):
        cols = pl.ds(pl.multiple_of(t * TILE, TILE), TILE)
        return [
            pltpu.make_async_copy(w.at[:, cols], ring.at[slot, :, pl.ds(j * TILE, TILE)], wsem.at[slot])
            for j, w in enumerate((wg_hbm, wu_hbm))
        ]

    def w_down(t, slot):
        return [
            pltpu.make_async_copy(
                wd_hbm.at[:, pl.ds(pl.multiple_of(t * pair + b * WIDE, WIDE), WIDE)],
                ring.at[slot, pl.ds(b * hidden, hidden), :],
                wsem.at[slot],
            )
            for b in range(2)
        ]

    def start(copies):
        for c in copies:
            c.start()

    def wait(copies):
        for c in copies:
            c.wait()

    def arrived(slot, n):
        block = ring.at[slot, pl.ds(0, n), :]
        pltpu.make_async_copy(block, block, wsem.at[slot]).wait()

    def to_part(u, b):
        s = u % SLOTS
        return rcopy(send0.at[s, b], recv0.at[s, b], s0.at[s, b], r0.at[s, b], part)

    def to_first(u, b):
        s = u % SLOTS
        return rcopy(send1.at[s, b], recv1.at[s, b], s1.at[s, b], r1.at[s, b], (xnb, ynb)[b])

    def to_second(u, b):
        s = u % SLOTS
        return rcopy(send2.at[s, b], recv2.at[s, b], s2.at[s, b], r2.at[s, b], (ynb, xnb)[b])

    def out_copy(u, b):
        cols = pl.ds(pl.multiple_of((u % downs) * pair + b * WIDE, WIDE), WIDE)
        at = pl.ds((u // downs) * rows, rows)
        return pltpu.make_async_copy(ost.at[u % 2, b], y_hbm.at[at, cols], osem.at[u % 2, b])

    def when(cond, f, *args):
        @pl.when(cond)
        def _():
            f(*args)

    def credit(sem, u, dev):
        @pl.when(u + SLOTS < sums)
        def _():
            pl.semaphore_signal(sem, inc=1, device_id={"tp": dev}, device_id_type=pl.DeviceIdType.MESH)

    def spend(sem, u):
        @pl.when(u >= SLOTS)
        def _():
            pl.semaphore_wait(sem, 1)

    def sum_first(u, b):
        s, o = u % SLOTS, u % OWN
        to_part(u, b).wait_recv()
        when(u >= SLOTS, lambda: to_first(u - SLOTS, b).wait_send())
        for blk in (0, (1, 2)[b]):
            acc[o, pl.ds(b * group + blk * rows, rows), :] += recv0[s, b, pl.ds(blk * rows, rows), :].astype(F32)
        for i, blk in enumerate(((2, 1)[b], 3)):
            total = acc[o, pl.ds(b * group + blk * rows, rows), :] + recv0[s, b, pl.ds(blk * rows, rows), :].astype(F32)
            send1[s, b, pl.ds(i * rows, rows), :] = total.astype(BF16)
        credit(free0.at[b], u, part)
        spend(free1.at[b], u)
        to_first(u, b).start()

    def sum_second(u, b):
        s, o = u % SLOTS, u % OWN
        to_first(u, b).wait_recv()
        when(u >= SLOTS, lambda: to_second(u - SLOTS, b).wait_send())
        keep = (1, 2)[b]
        acc[o, pl.ds(b * group, rows), :] += recv1[s, b, pl.ds(0, rows), :].astype(F32)
        total = acc[o, pl.ds(b * group + keep * rows, rows), :] + recv1[s, b, pl.ds(rows, rows), :].astype(F32)
        send2[s, b] = total.astype(BF16)
        credit(free1.at[b], u, (xnb, ynb)[b])
        spend(free2.at[b], u)
        to_second(u, b).start()

    def sum_last(u, b):
        s, o = u % SLOTS, u % OWN
        to_second(u, b).wait_recv()
        when(u >= 2, lambda: out_copy(u - 2, b).wait())
        total = acc[o, pl.ds(b * group, rows), :] + recv2[s, b].astype(F32)
        ost[u % 2, b] = total.astype(BF16)
        credit(free2.at[b], u, (ynb, xnb)[b])
        out_copy(u, b).start()

    def stages(v, lo, due):
        for stage, lag, b in due:
            u = v - lag
            when((u >= lo) & (u < lo + downs), stage, u, b)

    once = [(f, lag, b) for f, lag in ((sum_second, 7), (sum_first, 4), (sum_last, 10)) for b in range(2)]
    at_start = [(sum_second, 3, 1), (sum_first, 1, 0), (sum_last, 4, 1)]
    at_middle = [(sum_second, 2, 0), (sum_first, 1, 1), (sum_last, 3, 0)]

    def gated(gate, up):
        return (jax.nn.silu(gate) * up).astype(BF16)

    own = [
        pltpu.make_async_copy(x_hbm.at[pl.ds(h * rows, rows), cols], xv.at[h, pl.ds(0, rows), cols], xsem.at[i])
        for i, (h, cols) in enumerate(
            ((0, pl.ds(0, kcs[0])), (0, pl.ds(kcs[0], depth - kcs[0])), (1, pl.ds(0, depth)))
        )
    ]
    start(own[:1])
    barrier = pltpu.get_barrier_semaphore()
    for dev in (part, ynb, xnb):
        pl.semaphore_signal(barrier, inc=1, device_id={"tp": dev}, device_id_type=pl.DeviceIdType.MESH)
    start(own[1:])
    start(w_chunk(0, 0))
    wait(own[:1])
    pl.semaphore_wait(barrier, 3)
    gather_send(0, 0)
    wait(own[1:])
    gather_relay(0, 0)
    gather_send(0, 1)
    gather_send(0, 2)
    gather_diag(0, 0)
    gather_relay(0, 1)
    gather_send(0, 3)

    def chunk_comm(t):
        when(t + 1 < CHUNKS[0], gather_diag, 0, t + 1)
        when(t + 2 < CHUNKS[0], gather_relay, 0, t + 2)
        when(t + 4 < CHUNKS[0], gather_send, 0, t + 4)
        when(t % 3 == 1, gather_send, 1, t // 3)
        when((t % 3 == 0) & (t >= 3), gather_relay, 1, (t - 3) // 3)
        when((t % 3 == 2) & (t >= 5), gather_diag, 1, (t - 5) // 3)

    def chunk_product(t, slot, n):
        return jnp.dot(
            xv[0, :, pl.ds(pl.multiple_of(t * kcs[0], kcs[0]), kcs[0])],
            ring[slot, n * kcs[0] : (n + 1) * kcs[0], :],
            preferred_element_type=F32,
        )

    def chunk_trip(t, _):
        slot = t % 2
        chunk_comm(t)
        arrived(slot, 2 * blocks * kcs[0])
        start(w_chunk(t + 1, 1 - slot))
        gather_ready(0, t)
        for n in range(2 * blocks):
            acc[n] += chunk_product(t, slot, n)
        return 0

    final = CHUNKS[0] - 1
    arrived(0, 2 * blocks * kcs[0])
    start(w_chunk(1, 1))
    gather_ready(0, 0)
    for n in range(blocks):
        acc[n] = chunk_product(0, 0, n)
    chunk_comm(0)
    for n in range(blocks, 2 * blocks):
        acc[n] = chunk_product(0, 0, n)
    lax.fori_loop(1, final, chunk_trip, 0)
    chunk_comm(final)
    arrived(final % 2, 2 * blocks * kcs[0])
    start(w_down(0, 1 - final % 2))
    gather_ready(0, final)
    for n in range(blocks):
        gate = acc[n] + chunk_product(final, final % 2, n)
        up = acc[blocks + n] + chunk_product(final, final % 2, blocks + n)
        hid[:, n * WIDE : (n + 1) * WIDE] = gated(gate, up)
    base = CHUNKS[0]

    def full_tile(h, t, slot):
        r = jnp.dot(xv[h], ring[slot], preferred_element_type=F32)
        hid[:, pl.ds(pl.multiple_of(t * TILE, TILE), TILE)] = gated(r[:, :TILE], r[:, TILE:])

    def down_loop(h, base, lo):
        def trip(t, _):
            slot = (base + t) % 2
            u = lo + t
            stages(u, lo, at_start if h else once)
            if h == 0:
                when(t == 1, gather_diag, 1, 4)
                when(t < 3, gather_send, 1, 5 + t)
                when((t >= 2) & (t < 5), gather_relay, 1, 3 + t)
                when((t >= 4) & (t < 7), gather_diag, 1, 1 + t)
            arrived(slot, 2 * hidden)

            @pl.when(t + 1 < downs)
            def _():
                start(w_down(t + 1, 1 - slot))

            if h + 1 < HALVES:

                @pl.when(t + 1 == downs)
                def _():
                    start(w_full(0, 1 - slot))

            @pl.when(u >= SLOTS)
            def _():
                for b in range(2):
                    to_part(u - SLOTS, b).wait_send()
                    spend(free0.at[b], u)

            s, o = u % SLOTS, u % OWN
            for b in range(2):
                r = jnp.dot(hid[...], ring[slot, b * hidden : (b + 1) * hidden, :], preferred_element_type=F32)
                acc[o, pl.ds(b * group, group), :] = r[:group]
                send0[s, b] = r[group:].astype(BF16)
                if h:
                    to_part(u, b).start()
                    if b == 0:
                        stages(u, lo, at_middle)
            if not h:
                for b in range(2):
                    to_part(u, b).start()
            return 0

        lax.fori_loop(0, downs, trip, 0)

    down_loop(0, base, 0)
    base += downs

    def drain(c, _):
        gather_ready(1, c)
        return 0

    lax.fori_loop(0, CHUNKS[1], drain, 0)

    def full_trip(t, _):
        slot = (base + t) % 2
        stages(downs + t, 0, once)
        arrived(slot, depth)

        @pl.when(t + 1 < tiles)
        def _():
            start(w_full(t + 1, 1 - slot))

        @pl.when(t + 1 == tiles)
        def _():
            start(w_down(0, 1 - slot))

        full_tile(1, t, slot)
        return 0

    lax.fori_loop(0, tiles, full_trip, 0)
    down_loop(1, base + tiles, downs)

    def tail(v, _):
        stages(v, downs, at_start)
        stages(v, downs, at_middle)
        return 0

    lax.fori_loop(sums, sums + 4, tail, 0)

    for h in range(HALVES):

        def sent(c, _):
            gather_sent(h, c)
            return 0

        lax.fori_loop(0, CHUNKS[h], sent, 0)

    def last(u, _):
        for b in range(2):
            to_part(u, b).wait_send()
            to_first(u, b).wait_send()
            to_second(u, b).wait_send()
        return 0

    lax.fori_loop(sums - SLOTS, sums, last, 0)
    for u in (sums - 2, sums - 1):
        for b in range(2):
            out_copy(u, b).wait()


def solution(mesh):
    def step(x, w_gate, w_up, w_down):
        n = mesh.shape["tp"]
        rows, depth = x.shape
        hidden = w_gate.shape[1]
        m = n * rows // HALVES
        r = rows // HALVES
        gathers = sum(CHUNKS)
        blocks = 2 * hidden // WIDE
        dma = pltpu.SemaphoreType.DMA
        return pl.pallas_call(
            kernel,
            out_shape=jax.ShapeDtypeStruct((rows, depth), BF16),
            in_specs=[pl.BlockSpec(memory_space=pltpu.HBM)] * 4,
            out_specs=pl.BlockSpec(memory_space=pltpu.HBM),
            scratch_shapes=[
                pltpu.VMEM((HALVES, m, depth), BF16),
                pltpu.VMEM((m, hidden), BF16),
                pltpu.VMEM((2, depth, 2 * TILE), BF16),
                pltpu.VMEM((blocks, m, WIDE), F32),
                pltpu.VMEM((SLOTS, 2, 4 * r, WIDE), BF16),
                pltpu.VMEM((SLOTS, 2, 4 * r, WIDE), BF16),
                pltpu.VMEM((SLOTS, 2, 2 * r, WIDE), BF16),
                pltpu.VMEM((SLOTS, 2, 2 * r, WIDE), BF16),
                pltpu.VMEM((SLOTS, 2, r, WIDE), BF16),
                pltpu.VMEM((SLOTS, 2, r, WIDE), BF16),
                pltpu.VMEM((2, 2, r, WIDE), BF16),
                dma((2,)),
                dma((3,)),
                dma((2, 2)),
                dma((gathers, 8)),
                dma((gathers, 8)),
                dma((SLOTS, 2)),
                dma((SLOTS, 2)),
                dma((SLOTS, 2)),
                dma((SLOTS, 2)),
                dma((SLOTS, 2)),
                dma((SLOTS, 2)),
                pltpu.SemaphoreType.REGULAR((2,)),
                pltpu.SemaphoreType.REGULAR((2,)),
                pltpu.SemaphoreType.REGULAR((2,)),
            ],
            compiler_params=pltpu.CompilerParams(
                collective_id=0, has_side_effects=True, vmem_limit_bytes=67043328
            ),
        )(x, w_gate, w_up, w_down)

    return jax.shard_map(
        step,
        mesh=mesh,
        in_specs=(P(("dp", "tp"), None), P(None, "tp"), P(None, "tp"), P("tp", None)),
        out_specs=P(("dp", "tp"), None),
        check_vma=False,
    )
```

time: 420 us -> 233 us (0.55)
  Pallas kernels: 0 us -> 230 us
  matrix products: 210 us -> 0 us
  waiting for transfers between devices: 197 us -> 0 us
  between operations: 13.4 us -> 0.01 us
    pallas_call x0 -> x1, Pallas kernels: none -> 230 us  [step(): pl.pallas_call(kernel, out_shape=jax.ShapeDtypeStruct((rows, depth), BF16...]
    dot_general x3 -> x0, matrix products: 210 us -> none  [the longest x1 72.1 us: step(): up = jnp.dot(rows, w_up, preferred_element_type=jnp.float32)]
    reduce_scatter x1 -> x0, waiting for transfers between devices: 107 us -> none  [step(): return lax.psum_scatter(term, 'tp', scatter_dimension=0, tiled=True)]
    all_gather x1 -> x0, waiting for transfers between devices: 88.8 us -> none  [step(): rows = lax.all_gather(x, 'tp', axis=0, tiled=True)]
  transfers between devices with their start and end apart: 2 -> 0, of which waited for: 2 -> 0; matrix products, arithmetic and copies ran while one was open for 0% -> 0% of each run, Pallas kernels for 0% -> 0%
where the time goes in v2:
time: 233 us
  Pallas kernels  230 us (99%)
  local copies, waits for them, and re-layouts  3.1 us (1%)
    pallas_call x1, Pallas kernels, step(): pl.pallas_call(kernel, out_shape=jax.ShapeDtypeStruct((rows, depth), BF16...  230 us

profile of v2, /device:TPU:0, one launch (start us, length us, event | category | flops | bytes accessed | tf_op | source)
XLA Modules:
  0.0 232.9 jit_solution(14659831885621877614)
XLA Ops:
  0.0 229.8 %shard_map.46 = bf16[128,8192]{1,0:T(8,128)(2,1)} custom-call(bf16[128,8192]{1,0:T(8,128)(2,1)} %x_hbm.1, bf16[8192,3584]{1,0:T(8,128)(2,1)} %wg_hbm.1, bf16[8192,3584]{1,0:T(8,128)(2,1)} %wu_hbm.1, bf16[3584,8192]{1,0:T(8,128)(2,1)} %wd_hbm.1), custom_call_target="tpu_custom_call" | custom-call | tf_op jit(solution)/shard_map/pallas_call | solution.py:396
  229.8 3.1 %copy.6 = bf16[128,8192]{1,0:T(8,128)(2,1)} copy(bf16[128,8192]{1,0:T(8,128)(2,1)} %shard_map.46) | data formatting | bytes 4194304

commit v3 on v2

--- a/solution.py
+++ b/solution.py
@@ -11,7 +11,9 @@
 HALVES = 2
 TILE = 256
 WIDE = 512
+NARROW = WIDE // 2
 CHUNKS = (16, 8)
+MOVES = 8
 SLOTS = 5
 OWN = 12
 
@@ -137,13 +139,13 @@
         s = u % SLOTS
         return rcopy(send0.at[s, b], recv0.at[s, b], s0.at[s, b], r0.at[s, b], part)
 
-    def to_first(u, b):
-        s = u % SLOTS
-        return rcopy(send1.at[s, b], recv1.at[s, b], s1.at[s, b], r1.at[s, b], (xnb, ynb)[b])
-
-    def to_second(u, b):
-        s = u % SLOTS
-        return rcopy(send2.at[s, b], recv2.at[s, b], s2.at[s, b], r2.at[s, b], (ynb, xnb)[b])
+    def to_first(u, b, c):
+        s = u % SLOTS
+        return rcopy(send1.at[s, b, c], recv1.at[s, b, c], s1.at[s, b, c], r1.at[s, b, c], (xnb, ynb)[c])
+
+    def to_second(u, b, c):
+        s = u % SLOTS
+        return rcopy(send2.at[s, b, c], recv2.at[s, b, c], s2.at[s, b, c], r2.at[s, b, c], (ynb, xnb)[c])
 
     def out_copy(u, b):
         cols = pl.ds(pl.multiple_of((u % downs) * pair + b * WIDE, WIDE), WIDE)
@@ -165,39 +167,66 @@
         def _():
             pl.semaphore_wait(sem, 1)
 
+    def own_term(u, b, c, block):
+        return acc.at[u % OWN, pl.ds(b * group + block * rows, rows), pl.ds(c * NARROW, NARROW)]
+
     def sum_first(u, b):
-        s, o = u % SLOTS, u % OWN
+        s = u % SLOTS
         to_part(u, b).wait_recv()
-        when(u >= SLOTS, lambda: to_first(u - SLOTS, b).wait_send())
-        for blk in (0, (1, 2)[b]):
-            acc[o, pl.ds(b * group + blk * rows, rows), :] += recv0[s, b, pl.ds(blk * rows, rows), :].astype(F32)
-        for i, blk in enumerate(((2, 1)[b], 3)):
-            total = acc[o, pl.ds(b * group + blk * rows, rows), :] + recv0[s, b, pl.ds(blk * rows, rows), :].astype(F32)
-            send1[s, b, pl.ds(i * rows, rows), :] = total.astype(BF16)
+
+        @pl.when(u >= SLOTS)
+        def _():
+            for c in range(2):
+                to_first(u - SLOTS, b, c).wait_send()
+
+        for c in range(2):
+
+            def other(block):
+                return recv0[s, b, pl.ds(block * rows, rows), pl.ds(c * NARROW, NARROW)].astype(F32)
+
+            for i, block in enumerate(((2, 1)[c], 3)):
+                total = own_term(u, b, c, block)[...] + other(block)
+                send1[s, b, c, pl.ds(i * rows, rows), :] = total.astype(BF16)
+            for block in (0, (1, 2)[c]):
+                mine = own_term(u, b, c, block)
+                mine[...] = mine[...] + other(block)
+        for c in range(2):
+            spend(free1.at[b, c], u)
+            to_first(u, b, c).start()
         credit(free0.at[b], u, part)
-        spend(free1.at[b], u)
-        to_first(u, b).start()
 
     def sum_second(u, b):
-        s, o = u % SLOTS, u % OWN
-        to_first(u, b).wait_recv()
-        when(u >= SLOTS, lambda: to_second(u - SLOTS, b).wait_send())
-        keep = (1, 2)[b]
-        acc[o, pl.ds(b * group, rows), :] += recv1[s, b, pl.ds(0, rows), :].astype(F32)
-        total = acc[o, pl.ds(b * group + keep * rows, rows), :] + recv1[s, b, pl.ds(rows, rows), :].astype(F32)
-        send2[s, b] = total.astype(BF16)
-        credit(free1.at[b], u, (xnb, ynb)[b])
-        spend(free2.at[b], u)
-        to_second(u, b).start()
+        s = u % SLOTS
+        for c in range(2):
+            to_first(u, b, c).wait_recv()
+
+        @pl.when(u >= SLOTS)
+        def _():
+            for c in range(2):
+                to_second(u - SLOTS, b, c).wait_send()
+
+        for c in range(2):
+            total = own_term(u, b, c, (1, 2)[c])[...] + recv1[s, b, c, pl.ds(rows, rows), :].astype(F32)
+            send2[s, b, c] = total.astype(BF16)
+            mine = own_term(u, b, c, 0)
+            mine[...] = mine[...] + recv1[s, b, c, pl.ds(0, rows), :].astype(F32)
+        for c in range(2):
+            spend(free2.at[b, c], u)
+            to_second(u, b, c).start()
+        for c in range(2):
+            credit(free1.at[b, c], u, (xnb, ynb)[c])
 
     def sum_last(u, b):
-        s, o = u % SLOTS, u % OWN
-        to_second(u, b).wait_recv()
+        s = u % SLOTS
+        for c in range(2):
+            to_second(u, b, c).wait_recv()
         when(u >= 2, lambda: out_copy(u - 2, b).wait())
-        total = acc[o, pl.ds(b * group, rows), :] + recv2[s, b].astype(F32)
-        ost[u % 2, b] = total.astype(BF16)
-        credit(free2.at[b], u, (ynb, xnb)[b])
+        for c in range(2):
+            total = own_term(u, b, c, 0)[...] + recv2[s, b, c].astype(F32)
+            ost[u % 2, b, :, pl.ds(c * NARROW, NARROW)] = total.astype(BF16)
         out_copy(u, b).start()
+        for c in range(2):
+            credit(free2.at[b, c], u, (ynb, xnb)[c])
 
     def stages(v, lo, due):
         for stage, lag, b in due:
@@ -205,8 +234,7 @@
             when((u >= lo) & (u < lo + downs), stage, u, b)
 
     once = [(f, lag, b) for f, lag in ((sum_second, 7), (sum_first, 4), (sum_last, 10)) for b in range(2)]
-    at_start = [(sum_second, 3, 1), (sum_first, 1, 0), (sum_last, 4, 1)]
-    at_middle = [(sum_second, 2, 0), (sum_first, 1, 1), (sum_last, 3, 0)]
+    at_start, at_middle = ([(sum_first, 1, b), (sum_second, 2, b), (sum_last, 3, b)] for b in range(2))
 
     def gated(gate, up):
         return (jax.nn.silu(gate) * up).astype(BF16)
@@ -360,7 +388,7 @@
         stages(v, downs, at_middle)
         return 0
 
-    lax.fori_loop(sums, sums + 4, tail, 0)
+    lax.fori_loop(sums, sums + 3, tail, 0)
 
     for h in range(HALVES):
 
@@ -373,14 +401,30 @@
     def last(u, _):
         for b in range(2):
             to_part(u, b).wait_send()
-            to_first(u, b).wait_send()
-            to_second(u, b).wait_send()
+            for c in range(2):
+                to_first(u, b, c).wait_send()
+                to_second(u, b, c).wait_send()
         return 0
 
     lax.fori_loop(sums - SLOTS, sums, last, 0)
     for u in (sums - 2, sums - 1):
         for b in range(2):
             out_copy(u, b).wait()
+
+
+def move(src, dst, buf, sem):
+    n = sem.shape[1]
+    rows = src.shape[0] // n
+    at = [pl.ds(i * rows, rows) for i in range(n)]
+    into = [pltpu.make_async_copy(src.at[at[i]], buf.at[at[i]], sem.at[0, i]) for i in range(n)]
+    out = [pltpu.make_async_copy(buf.at[at[i]], dst.at[at[i]], sem.at[1, i]) for i in range(n)]
+    for c in into:
+        c.start()
+    for i in range(n):
+        into[i].wait()
+        out[i].start()
+    for c in out:
+        c.wait()
 
 
 def solution(mesh):
@@ -393,7 +437,7 @@
         gathers = sum(CHUNKS)
         blocks = 2 * hidden // WIDE
         dma = pltpu.SemaphoreType.DMA
-        return pl.pallas_call(
+        y = pl.pallas_call(
             kernel,
             out_shape=jax.ShapeDtypeStruct((rows, depth), BF16),
             in_specs=[pl.BlockSpec(memory_space=pltpu.HBM)] * 4,
@@ -405,10 +449,10 @@
                 pltpu.VMEM((blocks, m, WIDE), F32),
                 pltpu.VMEM((SLOTS, 2, 4 * r, WIDE), BF16),
                 pltpu.VMEM((SLOTS, 2, 4 * r, WIDE), BF16),
-                pltpu.VMEM((SLOTS, 2, 2 * r, WIDE), BF16),
-                pltpu.VMEM((SLOTS, 2, 2 * r, WIDE), BF16),
-                pltpu.VMEM((SLOTS, 2, r, WIDE), BF16),
-                pltpu.VMEM((SLOTS, 2, r, WIDE), BF16),
+                pltpu.VMEM((SLOTS, 2, 2, 2 * r, NARROW), BF16),
+                pltpu.VMEM((SLOTS, 2, 2, 2 * r, NARROW), BF16),
+                pltpu.VMEM((SLOTS, 2, 2, r, NARROW), BF16),
+                pltpu.VMEM((SLOTS, 2, 2, r, NARROW), BF16),
                 pltpu.VMEM((2, 2, r, WIDE), BF16),
                 dma((2,)),
                 dma((3,)),
@@ -417,18 +461,25 @@
                 dma((gathers, 8)),
                 dma((SLOTS, 2)),
                 dma((SLOTS, 2)),
-                dma((SLOTS, 2)),
-                dma((SLOTS, 2)),
-                dma((SLOTS, 2)),
-                dma((SLOTS, 2)),
+                dma((SLOTS, 2, 2)),
+                dma((SLOTS, 2, 2)),
+                dma((SLOTS, 2, 2)),
+                dma((SLOTS, 2, 2)),
                 pltpu.SemaphoreType.REGULAR((2,)),
-                pltpu.SemaphoreType.REGULAR((2,)),
-                pltpu.SemaphoreType.REGULAR((2,)),
+                pltpu.SemaphoreType.REGULAR((2, 2)),
+                pltpu.SemaphoreType.REGULAR((2, 2)),
             ],
             compiler_params=pltpu.CompilerParams(
                 collective_id=0, has_side_effects=True, vmem_limit_bytes=67043328
             ),
         )(x, w_gate, w_up, w_down)
+        return pl.pallas_call(
+            move,
+            out_shape=jax.ShapeDtypeStruct((rows, depth), BF16),
+            in_specs=[pl.BlockSpec(memory_space=pltpu.HBM)],
+            out_specs=pl.BlockSpec(memory_space=pltpu.HBM),
+            scratch_shapes=[pltpu.VMEM((rows, depth), BF16), dma((2, MOVES))],
+        )(y)
 
     return jax.shard_map(
         step,

time: 233 us -> 232 us (level)
  local copies, waits for them, and re-layouts: 3.1 us -> 0 us
    unnamed x1 -> x0, local copies, waits for them, and re-layouts: 3.1 us -> none
    pallas_call x0 -> x1, Pallas kernels: none -> 2.4 us  [step(): pl.pallas_call(move, out_shape=jax.ShapeDtypeStruct((rows, depth), BF16),...]
where the time goes in v3:
time: 232 us
  Pallas kernels  232 us (100%)
    pallas_call x1, Pallas kernels, step(): pl.pallas_call(kernel, out_shape=jax.ShapeDtypeStruct((rows, depth), BF16...  229 us

profile of v3, /device:TPU:0, one launch (start us, length us, event | category | flops | bytes accessed | tf_op | source)
XLA Modules:
  0.0 231.8 jit_solution(4781568361354114231)
XLA Ops:
  0.0 229.2 %shard_map.46.src = bf16[128,8192]{1,0:T(8,128)(2,1)} custom-call(bf16[128,8192]{1,0:T(8,128)(2,1)} %x_hbm.1, bf16[8192,3584]{1,0:T(8,128)(2,1)} %wg_hbm.1, bf16[8192,3584]{1,0:T(8,128)(2,1)} %wu_hbm.1, bf16[3584,8192]{1,0:T(8,128)(2,1)} %wd_hbm.1), custom_call_target="tpu_custom_call" | custom-call | tf_op jit(solution)/shard_map/pallas_call | solution.py:440
  229.2 2.4 %shard_map.47 = bf16[128,8192]{1,0:T(8,128)(2,1)} custom-call(bf16[128,8192]{1,0:T(8,128)(2,1)} %shard_map.46.src), custom_call_target="tpu_custom_call" | custom-call | tf_op jit(solution)/shard_map/pallas_call | solution.py:476
